TPU v7x, 1024 devices: a whole 4x4x32 slice. The times are simulated.
1024 devices in a mesh: grp: 4 (over x_hi, core), exc: 8 (over x_lo, y), col: 32 (over z).
Axes of the slice: x: 4 (x_hi: 2, x_lo: 2; x = x_hi * 2 + x_lo), y: 4, z: 32, core: 2. Of those that a mesh axis runs over, the one named last changes fastest.
Arguments:
- window_factor: float32 [1024, 32, 512], P('exc', 'grp'), may hold values from -0.375 to 0.375
- fitted_factor: float32 [1024, 512, 512], P('exc', 'col'), may hold values from -0.5 to 0.5
- pair_amps: float32 [16, 512, 512], P(None, 'col'), may hold values from -0.1875 to 0.1875
- cycle_amps: float32 [64, 32768], P(None, ('grp', 'exc')), may hold values from -6 to 6
- panel: float32 [32768, 4096], P(('grp', 'exc'), 'col'), may hold values from -0.03125 to 0.03125
Outputs:
- sigma: float32 [64, 4096], P(('grp', 'exc'), 'col')
All inputs are finite; a program needn't handle non-finite values.
Results may differ from a plain program's by a relative error of at most 0.0001.
Values sent between devices are 32-bit elements; how exact they have to be, the bound alone decides.
A program may use at most 64 MiB of HBM per device.

v0:
```python
import jax
import jax.numpy as jnp
from jax import lax
from jax.sharding import PartitionSpec as P

NI = 2
NJ = 8


def split_up(x, dim, size):
    shape = x.shape
    parts = x.reshape(*shape[:dim], size, shape[dim] // size, *shape[dim + 1 :])
    return jnp.moveaxis(parts, dim, 0)


def summed_on_arrival(x, axis, dim):
    parts = split_up(x, dim, lax.axis_size(axis))
    arrived = lax.all_to_all(parts, axis, split_axis=0, concat_axis=0, tiled=True)
    return arrived.sum(axis=0)


def shards(window_factor, fitted_factor, pair_amps, cycle_amps, panel):
    precise = lax.Precision.HIGHEST
    aux_count, virt_count, virtuals = window_factor.shape
    fit_count = fitted_factor.shape[1]
    amplitude = pair_amps.reshape(NI, NJ, fit_count, virtuals)
    inner = jnp.einsum("pac,ijdc->aijpd", window_factor, amplitude, precision=precise)
    inner_rows = inner.reshape(virt_count * NI * NJ, aux_count * fit_count)
    fitted_rows = fitted_factor.reshape(aux_count * fit_count, virtuals)
    ladder_terms = jnp.dot(
        inner_rows, fitted_rows, precision=precise, preferred_element_type=jnp.float32
    )
    ladder_terms = ladder_terms.reshape(virt_count * NI, NJ * virtuals)
    cycle_part = jnp.dot(cycle_amps, panel, precision=precise, preferred_element_type=jnp.float32)
    partial_value = summed_on_arrival(ladder_terms, "col", 1)
    offset = lax.axis_index("grp") * partial_value.shape[0]
    current = lax.dynamic_slice_in_dim(cycle_part, offset, partial_value.shape[0], 0)
    combined = lax.dynamic_update_slice_in_dim(cycle_part, current + partial_value, offset, 0)
    merged = summed_on_arrival(combined, ("grp", "exc"), 0)
    return merged


def solution(mesh):
    placed = (
        P("exc", "grp", None),
        P("exc", "col", None),
        P(None, "col", None),
        P(None, ("grp", "exc")),
        P(("grp", "exc"), "col"),
    )
    return jax.shard_map(
        shards, mesh=mesh, in_specs=placed, out_specs=P(("grp", "exc"), "col"), check_vma=False
    )
```

profile of v0, /device:TPU:1, one launch (start us, length us, event | category | flops | bytes accessed | tf_op | source)
XLA Modules:
  0.0 111.1 jit_solution(7540105853752464391)
XLA Ops:
  0.0 0.0 copy-start
  0.0 1.6 %copy-done = f32[128,8,512]{2,1,0:T(8,128)S(1)} copy-done((f32[128,8,512]{2,1,0:T(8,128)S(1)}, f32[128,8,512]{2,1,0:T(8,128)}, u32[]{:S(2)}) %copy-start) | copy-done | bytes 2097176
  1.6 4.0 %fusion.2 = f32[8,2,8,128,16]{3,4,0,2,1:T(8,128)S(1)} fusion(f32[2,8,16,512,1]{3,2,4,1,0:T(8,128)} %bitcast.22, f32[128,8,512,1,1]{2,1,0,4,3:T(8,128)S(1)} %bitcast.20), kind=kOutput, calls=%fused_computation.2 | convolution fusion | flops 1610612736 | bytes 3670016 | tf_op jit(solution)/shard_map/pac,ijdc->aijpd/dot_general | solution.py:27
  5.6 4.6 %copy.10 = f32[8,2,8,128,16]{4,3,2,1,0:T(8,128)} copy(f32[8,2,8,128,16]{3,4,0,2,1:T(8,128)S(1)} %fusion.2) | data formatting | bytes 2097152 | tf_op jit(solution)/shard_map/pac,ijdc->aijpd/transpose | solution.py:27
  10.3 7.9 %reshape.13 = f32[128,2048]{1,0:T(8,128)S(1)} reshape(f32[8,2,8,128,16]{4,3,2,1,0:T(8,128)} %copy.10) | data formatting | bytes 2097152 | tf_op jit(solution)/shard_map/reshape | solution.py:28
  18.1 4.6 %fusion.6 = f32[128,512]{1,0:T(8,128)S(1)} fusion(f32[128,2048]{1,0:T(8,128)S(1)} %reshape.13, f32[2048,512]{1,0:T(8,128)} %bitcast.21), kind=kOutput, calls=%fused_computation.6 | convolution fusion | flops 1610612736 | bytes 5505024 | tf_op jit(solution)/shard_map/dot_general | solution.py:30
  22.8 0.8 copy.21
  23.6 29.3 %all-to-all-start = ((f32[32,16,128]{2,1,0:T(8,128)}), f32[32,16,128]{2,1,0:T(8,128)S(1)}, u32[]{:S(2)}, u32[]{:S(2)}) async-start(f32[32,16,128]{2,1,0:T(8,128)} %bitcast.19), calls=%async_computation | async-start | bytes 524288 | tf_op jit(solution)/shard_map/all_to_all | solution.py:18
  52.9 1.6 %fusion.5 = f32[64,128]{1,0:T(8,128)S(1)} fusion(f32[64,1024]{1,0:T(8,128)} %param.8, f32[1024,128]{1,0:T(8,128)} %param.9), kind=kOutput, calls=%fused_computation.5 | convolution fusion | flops 100663296 | bytes 819200 | tf_op jit(solution)/shard_map/dot_general | solution.py:34
  54.5 39.0 %all-to-all-done = f32[32,16,128]{2,1,0:T(8,128)S(1)} async-done(((f32[32,16,128]{2,1,0:T(8,128)}), f32[32,16,128]{2,1,0:T(8,128)S(1)}, u32[]{:S(2)}, u32[]{:S(2)}) %all-to-all-start) | async-done | bytes 262176 | tf_op jit(solution)/shard_map/all_to_all | solution.py:18
  93.5 17.0 %all_to_all.10 = f32[32,2,128]{2,1,0:T(2,128)S(1)} all-to-all(f32[32,2,128]{2,1,0:T(2,128)S(1)} %bitcast.23), channel_id=1, replica_groups=mesh['grp'=4,'exc'=8,'col'=32] {'grp','exc'}, dimensions={0} | all-to-all | bytes 65536 | tf_op jit(solution)/shard_map/all_to_all | solution.py:18
  110.5 0.6 reduce_sum.19
  (3 shorter events, 0.1 us)
Async XLA Ops:
  0.0 1.6 %copy-start = (f32[128,8,512]{2,1,0:T(8,128)S(1)}, f32[128,8,512]{2,1,0:T(8,128)}, u32[]{:S(2)}) copy-start(f32[128,8,512]{2,1,0:T(8,128)} %param.5) | copy-start | bytes 6291460
  23.6 69.8 %all-to-all-start = ((f32[32,16,128]{2,1,0:T(8,128)}), f32[32,16,128]{2,1,0:T(8,128)S(1)}, u32[]{:S(2)}, u32[]{:S(2)}) async-start(f32[32,16,128]{2,1,0:T(8,128)} %bitcast.19), calls=%async_computation | async-start | bytes 524288 | tf_op jit(solution)/shard_map/all_to_all | solution.py:18
where the time goes:
time: 112 us; the launch traced here: 111 us
  waiting for transfers between devices  39 us (35%)
  starting transfers between devices  29.3 us (26%)
  blocking collectives  17 us (15%)
  local copies, waits for them, and re-layouts  14.9 us (13%)
  matrix products  10.2 us (9%)
    all_to_all x1, waiting for transfers between devices, summed_on_arrival(): lax.all_to_all(parts, axis, split_axis=0, concat_axis=0, tiled=True)  39 us
    all_to_all x1, starting transfers between devices, summed_on_arrival(): lax.all_to_all(parts, axis, split_axis=0, concat_axis=0, tiled=True)  29.3 us
    all_to_all x1, blocking collectives, summed_on_arrival(): lax.all_to_all(parts, axis, split_axis=0, concat_axis=0, tiled=True)  17 us
    reshape x1, local copies, waits for them, and re-layouts, shards(): inner_rows = inner.reshape(virt_count * NI * NJ, aux_count * fit_count)  7.87 us
    dot_general x1, matrix products, shards(): jnp.dot(inner_rows, fitted_rows, precision=precise, preferred_element_typ...  4.63 us
    transpose x1, local copies, waits for them, and re-layouts, shards(): jnp.einsum('pac,ijdc->aijpd', window_factor, amplitude, precision=precise)  4.62 us
    dot_general x1, matrix products, shards(): jnp.einsum('pac,ijdc->aijpd', window_factor, amplitude, precision=precise)  4.05 us
  transfers between devices with their start and end apart: 1, of which 1 were waited for; matrix products, arithmetic and copies ran while one was open for 1% of the time, Pallas kernels for 0%

commit v1 on v0

v1 whole, which is shorter than its diff:
```python
import jax
import jax.numpy as jnp
from jax import lax
from jax.experimental import pallas as pl
from jax.experimental.pallas import tpu as pltpu
from jax.sharding import PartitionSpec as P

MESH = pl.DeviceIdType.MESH
F32 = jnp.float32
BF16 = jnp.bfloat16
NI = 2
ORDER = (0, 1, 7, 2, 6, 3, 5, 4)


def halves(x):
    high = x.astype(BF16)
    return high, (x - high.astype(F32)).astype(BF16)


def product(a, b, contract):
    dims = (contract, ((), ()))

    def dot(u, v):
        return lax.dot_general(u, v, dims, preferred_element_type=F32)

    return dot(a[0], b[0]) + (dot(a[0], b[1]) + dot(a[1], b[0]))


def make_kernel(grps, excs, cols):
    def kernel(window, fitted, amps, cycle, panel, out, extra, wb, fb, ab, cb, pb, lh, ll, fh, fl,
               send1, recv1, csend1, crecv1, send2, recv2, csend2, crecv2,
               load, ss1, rs1, ssc1, rsc1, ss2, rs2, ssc2, rsc2, ready):
        g, e, z = lax.axis_index("grp"), lax.axis_index("exc"), lax.axis_index("col")
        aux, virts = window.shape[0], window.shape[1]
        pairs, fits = amps.shape[0], amps.shape[1]
        blocks = fitted.shape[2] // 128
        njs = pairs // NI

        loads = []
        for d in range(fits):
            loads.append(pltpu.make_async_copy(amps.at[:, d, :], ab.at[pl.ds(d * pairs, pairs), :], load.at[len(loads)]))
        for a in range(virts):
            loads.append(pltpu.make_async_copy(window.at[:, a, :], wb.at[pl.ds(a * aux, aux), :], load.at[len(loads)]))
        for d in range(fits):
            loads.append(pltpu.make_async_copy(fitted.at[:, d, :], fb.at[pl.ds(d * aux, aux), :], load.at[len(loads)]))
        loads.append(pltpu.make_async_copy(cycle, cb, load.at[len(loads)]))
        loads.append(pltpu.make_async_copy(panel, pb, load.at[len(loads)]))
        for c in loads:
            c.start()
        amp_loads, win_loads = loads[:fits], loads[fits : fits + virts]
        fit_loads, cyc_loads = loads[fits + virts : 2 * fits + virts], loads[2 * fits + virts :]

        barrier = pltpu.get_barrier_semaphore()
        near = [{"exc": e ^ k} for k in range(1, excs)] + [{"grp": g ^ k} for k in range(1, grps)]
        for peer in near:
            pl.semaphore_signal(barrier, inc=1, device_id=peer, device_id_type=MESH)

        @pl.loop(z + 1, cols)
        def _(p):
            pl.semaphore_signal(barrier, inc=1, device_id={"col": p}, device_id_type=MESH)

        for c in amp_loads:
            c.wait()
        amp = halves(ab[...])
        for a in range(0, virts, 2):
            win_loads[a].wait()
            win_loads[a + 1].wait()
            win = halves(wb[pl.ds(a * aux, 2 * aux), :])
            inner = product(amp, win, ((1,), (1,)))
            for s in range(2):
                for d in range(fits):
                    high, low = halves(inner[d * pairs : (d + 1) * pairs, s * aux : (s + 1) * aux])
                    rows, lanes = pl.ds((a + s) * pairs, pairs), pl.ds(d * aux, aux)
                    lh[rows, lanes] = high
                    ll[rows, lanes] = low

        for d in range(fits):
            fit_loads[d].wait()
            high, low = halves(fb[pl.ds(d * aux, aux), :])
            fh[pl.ds(d * aux, aux), :] = high
            fl[pl.ds(d * aux, aux), :] = low
        for n in range(0, blocks, 2):
            lanes = pl.ds(n * 128, 256)
            terms = product((lh[...], ll[...]), (fh[:, lanes], fl[:, lanes]), ((1,), (0,)))
            for q in range(excs):
                for s in range(2):
                    for i in range(NI):
                        row = q * pairs + i * njs
                        send1[pl.ds(q * njs, njs), (n + s) * NI + i, :] = terms[row : row + njs, s * 128 : (s + 1) * 128]

        pl.semaphore_wait(barrier, len(near) + z)

        first = []
        js = [lax.rem(z // blocks + (njs // 2 + t), njs) for t in ORDER]
        for p, j in enumerate(js):
            step = []
            for k in reversed(range(1, excs)):
                c = pltpu.make_async_remote_copy(send1.at[(e ^ k) * njs + j], recv1.at[k - 1, p], ss1.at[k - 1, p], rs1.at[k - 1, p],
                                                 device_id={"exc": e ^ k}, device_id_type=MESH)
                c.start()
                step.append(c)
            first.append(step)

        @pl.loop(0, z)
        def _(p):
            pl.semaphore_signal(ready, inc=1, device_id={"col": p}, device_id_type=MESH)

        for c in cyc_loads:
            c.wait()
        part = product(halves(cb[...]), halves(pb[...]), ((1,), (0,)))
        for q in range(excs):
            for h in range(grps):
                row = (h * excs + q) * NI
                csend1[q, pl.ds(h * NI, NI), :] = part[row : row + NI, :]
        step = []
        for k in reversed(range(1, excs)):
            c = pltpu.make_async_remote_copy(csend1.at[e ^ k], crecv1.at[k - 1], ssc1.at[k - 1], rsc1.at[k - 1],
                                             device_id={"exc": e ^ k}, device_id_type=MESH)
            c.start()
            step.append(c)
        first.append(step)

        def to_col(p):
            return pltpu.make_async_remote_copy(send2.at[p], recv2.at[z], ss2.at[p], rs2.at[z],
                                                device_id={"col": p}, device_id_type=MESH)

        for p, j in enumerate(js):
            for c in first[p]:
                c.wait_recv()
            total = send1[e * njs + j]
            for k in range(1, excs):
                total = total + recv1[k - 1, p]
            for n in range(blocks):
                to = j * blocks + n
                send2[to] = total[n * NI : (n + 1) * NI, :]

                @pl.when(to < z)
                def _():
                    to_col(to).start()

        for c in first[-1]:
            c.wait_recv()
        total = csend1[e]
        for k in range(1, excs):
            total = total + crecv1[k - 1]
        for h in range(grps):
            csend2[h] = total[h * NI : (h + 1) * NI, :]
        across = []
        for k in range(1, grps):
            c = pltpu.make_async_remote_copy(csend2.at[g ^ k], crecv2.at[k - 1], ssc2.at[k - 1], rsc2.at[k - 1],
                                             device_id={"grp": g ^ k}, device_id_type=MESH)
            c.start()
            across.append(c)

        @pl.when(z < cols - 1)
        def _():
            pl.semaphore_wait(ready, cols - 1 - z)

        @pl.loop(z + 1, cols)
        def _(p):
            to_col(p).start()

        for c in across:
            c.wait_recv()
        cyc = csend2[g]
        for k in range(1, grps):
            cyc = cyc + crecv2[k - 1]
        extra[...] = cyc

        def arrived(p):
            return pltpu.make_async_remote_copy(send2.at[p], recv2.at[p], ss2.at[p], rs2.at[p],
                                                device_id={"col": p}, device_id_type=MESH)

        result = send2[z]
        for k in range(1, cols):
            p = lax.rem(z + k, cols)
            arrived(p).wait_recv()
            result = result + recv2[p]
        out[...] = result
        for step in first + [across]:
            for c in step:
                c.wait_send()
        for k in range(1, cols):
            arrived(lax.rem(z + k, cols)).wait_send()

    return kernel


def solution(mesh):
    grps, excs, cols = mesh.shape["grp"], mesh.shape["exc"], mesh.shape["col"]

    def shards(window, fitted, amps, cycle, panel):
        aux, virts, virtuals = window.shape
        fits, wide = fitted.shape[1:]
        pairs = amps.shape[0]
        njs, blocks = pairs // NI, wide // 128
        DMA = pltpu.SemaphoreType.DMA
        scratch = [
            pltpu.VMEM((virts * aux, virtuals), F32),
            pltpu.VMEM((fits * aux, wide), F32),
            pltpu.VMEM((fits * pairs, virtuals), F32),
            pltpu.VMEM(cycle.shape, F32),
            pltpu.VMEM(panel.shape, F32),
            pltpu.VMEM((virts * pairs, fits * aux), BF16),
            pltpu.VMEM((virts * pairs, fits * aux), BF16),
            pltpu.VMEM((fits * aux, wide), BF16),
            pltpu.VMEM((fits * aux, wide), BF16),
            pltpu.VMEM((excs * njs, blocks * NI, 128), F32),
            pltpu.VMEM((excs - 1, njs, blocks * NI, 128), F32),
            pltpu.VMEM((excs, grps * NI, 128), F32),
            pltpu.VMEM((excs - 1, grps * NI, 128), F32),
            pltpu.VMEM((cols, NI, 128), F32),
            pltpu.VMEM((cols, NI, 128), F32),
            pltpu.VMEM((grps, NI, 128), F32),
            pltpu.VMEM((grps - 1, NI, 128), F32),
            DMA((2 * fits + virts + 2,)),
            DMA((excs - 1, njs)),
            DMA((excs - 1, njs)),
            DMA((excs - 1,)),
            DMA((excs - 1,)),
            DMA((cols,)),
            DMA((cols,)),
            DMA((grps - 1,)),
            DMA((grps - 1,)),
            pltpu.SemaphoreType.REGULAR,
        ]
        anywhere = pl.BlockSpec(memory_space=pl.ANY)
        ladder, cyc = pl.pallas_call(
            make_kernel(grps, excs, cols),
            out_shape=(jax.ShapeDtypeStruct((NI, 128), F32),) * 2,
            in_specs=[anywhere] * 5,
            out_specs=(pl.BlockSpec(memory_space=pltpu.VMEM),) * 2,
            scratch_shapes=scratch,
            compiler_params=pltpu.CompilerParams(collective_id=0, has_side_effects=True),
            name="residual",
        )(window, fitted, amps, cycle, panel)
        return ladder + cyc

    placed = (
        P("exc", "grp", None),
        P("exc", "col", None),
        P(None, "col", None),
        P(None, ("grp", "exc")),
        P(("grp", "exc"), "col"),
    )
    return jax.shard_map(
        shards, mesh=mesh, in_specs=placed, out_specs=P(("grp", "exc"), "col"), check_vma=False
    )
```

time: 112 us -> 44.7 us (0.40)
  Pallas kernels: 0 us -> 42.7 us
  waiting for transfers between devices: 39 us -> 0 us
  starting transfers between devices: 29.3 us -> 0 us
  blocking collectives: 17 us -> 0 us
  local copies, waits for them, and re-layouts: 14.9 us -> 0 us
  matrix products: 10.2 us -> 0 us
    pallas_call x0 -> x1, Pallas kernels: none -> 42.7 us  [shards(): pl.pallas_call(make_kernel(grps, excs, cols), out_shape=(jax.ShapeDtypeSt...]
    all_to_all x1 -> x0, waiting for transfers between devices: 39 us -> none  [summed_on_arrival(): lax.all_to_all(parts, axis, split_axis=0, concat_axis=0, tiled=True)]
    all_to_all x1 -> x0, starting transfers between devices: 29.3 us -> none  [summed_on_arrival(): lax.all_to_all(parts, axis, split_axis=0, concat_axis=0, tiled=True)]
    all_to_all x1 -> x0, blocking collectives: 17 us -> none  [summed_on_arrival(): lax.all_to_all(parts, axis, split_axis=0, concat_axis=0, tiled=True)]
    dot_general x3 -> x0, matrix products: 10.2 us -> none  [the longest x1 4.63 us: shards(): jnp.dot(inner_rows, fitted_rows, precision=precise, preferred_element_typ...]
    reshape x1 -> x0, local copies, waits for them, and re-layouts: 7.87 us -> none  [shards(): inner_rows = inner.reshape(virt_count * NI * NJ, aux_count * fit_count)]
    transpose x1 -> x0, local copies, waits for them, and re-layouts: 4.62 us -> none  [shards(): jnp.einsum('pac,ijdc->aijpd', window_factor, amplitude, precision=precise)]
    unnamed x2 -> x0, local copies, waits for them, and re-layouts: 1.59 us -> none
  transfers between devices with their start and end apart: 1 -> 0, of which waited for: 1 -> 0; matrix products, arithmetic and copies ran while one was open for 1% -> 0% of each run, Pallas kernels for 0% -> 0%
where the time goes in v1:
time: 44.7 us; the launch traced here: 43.9 us
  Pallas kernels  42.7 us (96%)
  other arithmetic  1.23 us (3%)
    pallas_call x1, Pallas kernels, shards(): pl.pallas_call(make_kernel(grps, excs, cols), out_shape=(jax.ShapeDtypeSt...  42.7 us
    add x1, other arithmetic, shards(): return ladder + cyc  1.23 us

profile of v1, /device:TPU:1, one launch (start us, length us, event | category | flops | bytes accessed | tf_op | source)
XLA Modules:
  0.0 43.9 jit_solution(4570634941355453016)
XLA Ops:
  0.0 42.7 %residual.1 = (f32[2,128]{1,0:T(2,128)}, f32[2,128]{1,0:T(2,128)}) custom-call(f32[128,8,512]{2,1,0:T(8,128)} %window.1, f32[128,16,512]{2,1,0:T(8,128)} %fitted.1, f32[16,16,512]{2,1,0:T(8,128)} %amps.1, f32[64,1024]{1,0:T(8,128)} %cycle.1, f32[1024,128]{1,0:T(8,128)} %panel.1), custom_call_target="tpu_custom_call" | custom-call | tf_op jit(solution)/shard_map/residual/pallas_call | solution.py:228
  42.7 1.2 %add.3 = f32[2,128]{1,0:T(2,128)} add(f32[2,128]{1,0:T(2,128)} %get-tuple-element.7, f32[2,128]{1,0:T(2,128)} %get-tuple-element.8) | non-fusion elementwise | flops 256 | bytes 3072 | tf_op jit(solution)/shard_map/add | solution.py:237

commit v2 on v1

v2 whole, which is shorter than its diff:
```python
import jax
import jax.numpy as jnp
from jax import lax
from jax.experimental import pallas as pl
from jax.experimental.pallas import tpu as pltpu
from jax.sharding import PartitionSpec as P

MESH = pl.DeviceIdType.MESH
F32 = jnp.float32
BF16 = jnp.bfloat16
NI = 2
GROUPS = ((0, 4), (4, 4), (8, 4), (12, 2), (14, 2))
ORDER = (0, 1, 7, 2, 6, 3, 5, 4)


def halves(x):
    high = x.astype(BF16)
    return high, (x - high.astype(F32)).astype(BF16)


def product(a, b, contract):
    dims = (contract, ((), ()))

    def dot(u, v):
        return lax.dot_general(u, v, dims, preferred_element_type=F32)

    return dot(a[0], b[0]) + (dot(a[0], b[1]) + dot(a[1], b[0]))


def make_kernel(grps, excs, cols):
    def kernel(window, fitted, amps, cycle, panel, out, extra, wb, fb, ab, cb, pb, lh, ll, acc,
               send1, recv1, csend1, crecv1, send2, recv2, csend2, crecv2,
               amp_load, win_load, fit_load, cyc_load, sent, rs1, rsc, rs2, ready):
        g, e, z = lax.axis_index("grp"), lax.axis_index("exc"), lax.axis_index("col")
        aux, virts = window.shape[0], window.shape[1]
        pairs, fits = amps.shape[0], amps.shape[1]
        blocks = fitted.shape[2] // 128
        njs = pairs // NI

        def landed(ref, sem):
            return pltpu.make_async_copy(ref, ref, sem)

        for d in range(fits):
            pltpu.make_async_copy(amps.at[:, d, :], ab.at[pl.ds(d * pairs, pairs), :], amp_load).start()
        for a in range(virts):
            pltpu.make_async_copy(window.at[:, a, :], wb.at[pl.ds(a * aux, aux), :], win_load.at[a // 2]).start()
        for t, (d0, nd) in enumerate(GROUPS):
            for d in range(d0, d0 + nd):
                pltpu.make_async_copy(fitted.at[:, d, :], fb.at[pl.ds(d * aux, aux), :], fit_load.at[t]).start()
        pltpu.make_async_copy(cycle, cb, cyc_load.at[0]).start()
        pltpu.make_async_copy(panel, pb, cyc_load.at[1]).start()

        barrier = pltpu.get_barrier_semaphore()
        near = [{"exc": e ^ k} for k in range(1, excs)] + [{"grp": g ^ k} for k in range(1, grps)]
        for peer in near:
            pl.semaphore_signal(barrier, inc=1, device_id=peer, device_id_type=MESH)

        @pl.loop(z + 1, cols)
        def _(p):
            pl.semaphore_signal(barrier, inc=1, device_id={"col": p}, device_id_type=MESH)

        landed(ab, amp_load).wait()
        amp = halves(ab[...])
        for a in range(0, virts, 2):
            both = pl.ds(a * aux, 2 * aux)
            landed(wb.at[both, :], win_load.at[a // 2]).wait()
            inner = product(amp, halves(wb[both, :]), ((1,), (1,)))
            for s in range(2):
                for d in range(fits):
                    high, low = halves(inner[d * pairs : (d + 1) * pairs, s * aux : (s + 1) * aux])
                    rows, lanes = pl.ds((a + s) * pairs, pairs), pl.ds(d * aux, aux)
                    lh[rows, lanes] = high
                    ll[rows, lanes] = low

        for t, (d0, nd) in enumerate(GROUPS):
            deep = pl.ds(d0 * aux, nd * aux)
            landed(fb.at[deep, :], fit_load.at[t]).wait()
            for n in range(0, blocks, 2):
                lanes = pl.ds(n * 128, 256)
                terms = product((lh[:, deep], ll[:, deep]), halves(fb[deep, lanes]), ((1,), (0,)))
                if t:
                    terms = terms + acc[:, lanes]
                if t < len(GROUPS) - 1:
                    acc[:, lanes] = terms
                    continue
                for q in range(excs):
                    for s in range(2):
                        for i in range(NI):
                            row = q * pairs + i * njs
                            send1[pl.ds(q * njs, njs), (n + s) * NI + i, :] = terms[row : row + njs, s * 128 : (s + 1) * 128]

        pl.semaphore_wait(barrier, len(near) + z)

        js = [lax.rem(z // blocks + (njs // 2 + t), njs) for t in ORDER]
        for p, j in enumerate(js):
            for k in reversed(range(1, excs)):
                pltpu.make_async_remote_copy(send1.at[(e ^ k) * njs + j], recv1.at[p, k - 1], sent.at[0], rs1.at[p],
                                             device_id={"exc": e ^ k}, device_id_type=MESH).start()

        @pl.loop(0, z)
        def _(p):
            pl.semaphore_signal(ready, inc=1, device_id={"col": p}, device_id_type=MESH)

        landed(cb, cyc_load.at[0]).wait()
        landed(pb, cyc_load.at[1]).wait()
        part = product(halves(cb[...]), halves(pb[...]), ((1,), (0,)))
        for q in range(excs):
            for h in range(grps):
                row = (h * excs + q) * NI
                csend1[q, pl.ds(h * NI, NI), :] = part[row : row + NI, :]
        for k in reversed(range(1, excs)):
            pltpu.make_async_remote_copy(csend1.at[e ^ k], crecv1.at[k - 1], sent.at[1], rsc.at[0],
                                         device_id={"exc": e ^ k}, device_id_type=MESH).start()

        def to_col(p):
            return pltpu.make_async_remote_copy(send2.at[p], recv2.at[lax.rem(p - z - 1 + cols, cols)], sent.at[2], rs2,
                                                device_id={"col": p}, device_id_type=MESH)

        for p, j in enumerate(js):
            landed(recv1.at[p], rs1.at[p]).wait()
            total = send1[e * njs + j]
            for k in range(1, excs):
                total = total + recv1[p, k - 1]
            for n in range(blocks):
                to = j * blocks + n
                send2[to] = total[n * NI : (n + 1) * NI, :]

                @pl.when(to < z)
                def _():
                    to_col(to).start()

        landed(crecv1, rsc.at[0]).wait()
        total = csend1[e]
        for k in range(1, excs):
            total = total + crecv1[k - 1]
        for h in range(grps):
            csend2[h] = total[h * NI : (h + 1) * NI, :]
        for k in range(1, grps):
            pltpu.make_async_remote_copy(csend2.at[g ^ k], crecv2.at[k - 1], sent.at[3], rsc.at[1],
                                         device_id={"grp": g ^ k}, device_id_type=MESH).start()

        @pl.when(z < cols - 1)
        def _():
            pl.semaphore_wait(ready, cols - 1 - z)

        @pl.loop(z + 1, cols)
        def _(p):
            to_col(p).start()

        landed(crecv2, rsc.at[1]).wait()
        cyc = csend2[g]
        for k in range(1, grps):
            cyc = cyc + crecv2[k - 1]
        extra[...] = cyc
        for t, (ref, own) in enumerate(((send1, njs), (csend1, 1), (send2, 1), (csend2, 1))):
            landed(ref.at[pl.ds(0, ref.shape[0] - own)], sent.at[t]).wait()
        landed(recv2, rs2).wait()
        result = send2[z]
        for k in range(1, cols):
            result = result + recv2[k - 1]
        out[...] = result

    return kernel


def solution(mesh):
    grps, excs, cols = mesh.shape["grp"], mesh.shape["exc"], mesh.shape["col"]

    def shards(window, fitted, amps, cycle, panel):
        aux, virts, virtuals = window.shape
        fits, wide = fitted.shape[1:]
        pairs = amps.shape[0]
        njs, blocks = pairs // NI, wide // 128
        DMA = pltpu.SemaphoreType.DMA
        scratch = [
            pltpu.VMEM((virts * aux, virtuals), F32),
            pltpu.VMEM((fits * aux, wide), F32),
            pltpu.VMEM((fits * pairs, virtuals), F32),
            pltpu.VMEM(cycle.shape, F32),
            pltpu.VMEM(panel.shape, F32),
            pltpu.VMEM((virts * pairs, fits * aux), BF16),
            pltpu.VMEM((virts * pairs, fits * aux), BF16),
            pltpu.VMEM((virts * pairs, wide), F32),
            pltpu.VMEM((excs * njs, blocks * NI, 128), F32),
            pltpu.VMEM((njs, excs - 1, blocks * NI, 128), F32),
            pltpu.VMEM((excs, grps * NI, 128), F32),
            pltpu.VMEM((excs - 1, grps * NI, 128), F32),
            pltpu.VMEM((cols, NI, 128), F32),
            pltpu.VMEM((cols - 1, NI, 128), F32),
            pltpu.VMEM((grps, NI, 128), F32),
            pltpu.VMEM((grps - 1, NI, 128), F32),
            DMA,
            DMA((virts // 2,)),
            DMA((len(GROUPS),)),
            DMA((2,)),
            DMA((4,)),
            DMA((njs,)),
            DMA((2,)),
            DMA,
            pltpu.SemaphoreType.REGULAR,
        ]
        anywhere = pl.BlockSpec(memory_space=pl.ANY)
        ladder, cyc = pl.pallas_call(
            make_kernel(grps, excs, cols),
            out_shape=(pltpu.VMEM((NI, 128), F32),) * 2,
            in_specs=[anywhere] * 5,
            out_specs=(pl.BlockSpec(memory_space=pltpu.VMEM),) * 2,
            scratch_shapes=scratch,
            compiler_params=pltpu.CompilerParams(collective_id=0, has_side_effects=True),
            name="residual",
        )(window, fitted, amps, cycle, panel)
        return ladder + cyc

    placed = (
        P("exc", "grp", None),
        P("exc", "col", None),
        P(None, "col", None),
        P(None, ("grp", "exc")),
        P(("grp", "exc"), "col"),
    )
    return jax.shard_map(
        shards, mesh=mesh, in_specs=placed, out_specs=P(("grp", "exc"), "col"), check_vma=False
    )
```

time: 44.7 us -> 41.2 us (0.922)
  Pallas kernels: 42.7 us -> 39.8 us
  other arithmetic: 1.23 us -> 0.57 us
    pallas_call x1, Pallas kernels: 42.7 us -> 39.8 us  [shards(): pl.pallas_call(make_kernel(grps, excs, cols), out_shape=(pltpu.VMEM((NI,...]
    add x1, other arithmetic: 1.23 us -> 0.57 us  [shards(): return ladder + cyc]
where the time goes in v2:
time: 41.2 us; the launch traced here: 40.4 us
  Pallas kernels  39.8 us (97%)
  other arithmetic  0.57 us (1%)
    pallas_call x1, Pallas kernels, shards(): pl.pallas_call(make_kernel(grps, excs, cols), out_shape=(pltpu.VMEM((NI,...  39.8 us

profile of v2, /device:TPU:1, one launch (start us, length us, event | category | flops | bytes accessed | tf_op | source)
XLA Modules:
  0.0 40.4 jit_solution(13831150946652205105)
XLA Ops:
  0.0 39.8 %residual.1 = (f32[2,128]{1,0:T(2,128)S(1)}, f32[2,128]{1,0:T(2,128)S(1)}) custom-call(f32[128,8,512]{2,1,0:T(8,128)} %window.1, f32[128,16,512]{2,1,0:T(8,128)} %fitted.1, f32[16,16,512]{2,1,0:T(8,128)} %amps.1, f32[64,1024]{1,0:T(8,128)} %cycle.1, f32[1024,128]{1,0:T(8,128)} %panel.1), custom_call_target="tpu_custom_call" | custom-call | tf_op jit(solution)/shard_map/residual/pallas_call | solution.py:203
  39.8 0.6 %add.3 = f32[2,128]{1,0:T(2,128)} add(f32[2,128]{1,0:T(2,128)S(1)} %get-tuple-element.7, f32[2,128]{1,0:T(2,128)S(1)} %get-tuple-element.8) | non-fusion elementwise | flops 256 | bytes 3072 | tf_op jit(solution)/shard_map/add | solution.py:212

commit v3 on v2

--- a/solution.py
+++ b/solution.py
@@ -29,8 +29,8 @@
 
 def make_kernel(grps, excs, cols):
     def kernel(window, fitted, amps, cycle, panel, out, extra, wb, fb, ab, cb, pb, lh, ll, acc,
-               send1, recv1, csend1, crecv1, send2, recv2, csend2, crecv2,
-               amp_load, win_load, fit_load, cyc_load, sent, rs1, rsc, rs2, ready):
+               send1, recv1, csend1, crecv1, send2, recv2, csend2, crecv2, direct,
+               amp_load, win_load, fit_load, cyc_load, sent, rs1, rsc, rs2, rsd, ready):
         g, e, z = lax.axis_index("grp"), lax.axis_index("exc"), lax.axis_index("col")
         aux, virts = window.shape[0], window.shape[1]
         pairs, fits = amps.shape[0], amps.shape[1]
@@ -50,14 +50,28 @@
         pltpu.make_async_copy(cycle, cb, cyc_load.at[0]).start()
         pltpu.make_async_copy(panel, pb, cyc_load.at[1]).start()
 
+        half = cols // 2
+        lower = z < half
+        known = jnp.minimum(z, half)
         barrier = pltpu.get_barrier_semaphore()
         near = [{"exc": e ^ k} for k in range(1, excs)] + [{"grp": g ^ k} for k in range(1, grps)]
         for peer in near:
             pl.semaphore_signal(barrier, inc=1, device_id=peer, device_id_type=MESH)
 
-        @pl.loop(z + 1, cols)
-        def _(p):
-            pl.semaphore_signal(barrier, inc=1, device_id={"col": p}, device_id_type=MESH)
+        source = (z >= half) & (z < half + blocks)
+        target = z < blocks
+
+        @pl.when(target)
+        def _():
+            for k in range(1, excs):
+                for t in range(blocks):
+                    pl.semaphore_signal(barrier, inc=1, device_id={"exc": e ^ k, "col": half + t}, device_id_type=MESH)
+
+        @pl.when(lower)
+        def _():
+            @pl.loop(z + 1, cols)
+            def _(p):
+                pl.semaphore_signal(barrier, inc=1, device_id={"col": p}, device_id_type=MESH)
 
         landed(ab, amp_load).wait()
         amp = halves(ab[...])
@@ -89,15 +103,30 @@
                             row = q * pairs + i * njs
                             send1[pl.ds(q * njs, njs), (n + s) * NI + i, :] = terms[row : row + njs, s * 128 : (s + 1) * 128]
 
-        pl.semaphore_wait(barrier, len(near) + z)
-
-        js = [lax.rem(z // blocks + (njs // 2 + t), njs) for t in ORDER]
-        for p, j in enumerate(js):
+        pl.semaphore_wait(barrier, len(near) + known + jnp.where(source, (excs - 1) * blocks, 0))
+
+        @pl.when(source)
+        def _():
+            for t in range(blocks):
+                for k in reversed(range(excs)):
+                    pltpu.make_async_remote_copy(send1.at[(e ^ k) * njs, pl.ds(t * NI, NI), :], direct.at[(z - half) * excs + e],
+                                                 sent.at[4], rsd, device_id={"exc": e ^ k, "col": t}, device_id_type=MESH).start()
+
+        def to_exc(p, j):
             for k in reversed(range(1, excs)):
                 pltpu.make_async_remote_copy(send1.at[(e ^ k) * njs + j], recv1.at[p, k - 1], sent.at[0], rs1.at[p],
                                              device_id={"exc": e ^ k}, device_id_type=MESH).start()
 
-        @pl.loop(0, z)
+        js = [lax.rem(z // blocks + (njs // 2 + t), njs) for t in ORDER]
+
+        @pl.when(jnp.logical_not(source))
+        def _():
+            to_exc(0, js[0])
+
+        for p in range(1, njs):
+            to_exc(p, js[p])
+
+        @pl.loop(0, known)
         def _(p):
             pl.semaphore_signal(ready, inc=1, device_id={"col": p}, device_id_type=MESH)
 
@@ -116,7 +145,7 @@
             return pltpu.make_async_remote_copy(send2.at[p], recv2.at[lax.rem(p - z - 1 + cols, cols)], sent.at[2], rs2,
                                                 device_id={"col": p}, device_id_type=MESH)
 
-        for p, j in enumerate(js):
+        def reduce_to_cols(p, j):
             landed(recv1.at[p], rs1.at[p]).wait()
             total = send1[e * njs + j]
             for k in range(1, excs):
@@ -125,9 +154,16 @@
                 to = j * blocks + n
                 send2[to] = total[n * NI : (n + 1) * NI, :]
 
-                @pl.when(to < z)
+                @pl.when(to < known)
                 def _():
                     to_col(to).start()
+
+        @pl.when(jnp.logical_not(source))
+        def _():
+            reduce_to_cols(0, js[0])
+
+        for p in range(1, njs):
+            reduce_to_cols(p, js[p])
 
         landed(crecv1, rsc.at[0]).wait()
         total = csend1[e]
@@ -139,22 +175,57 @@
             pltpu.make_async_remote_copy(csend2.at[g ^ k], crecv2.at[k - 1], sent.at[3], rsc.at[1],
                                          device_id={"grp": g ^ k}, device_id_type=MESH).start()
 
-        @pl.when(z < cols - 1)
-        def _():
-            pl.semaphore_wait(ready, cols - 1 - z)
-
-        @pl.loop(z + 1, cols)
+        pl.semaphore_wait(ready, jnp.where(lower, cols - 1 - z, 1))
+        for teller, start in ((half - 1, half), (0, half + half // 2)):
+
+            @pl.when(z == teller)
+            def _():
+                @pl.loop(start, start + half // 2)
+                def _(p):
+                    pl.semaphore_signal(ready, inc=1, device_id={"col": p}, device_id_type=MESH)
+
+        @pl.loop(jnp.where(lower, z + 1, half), cols)
         def _(p):
-            to_col(p).start()
+            @pl.when(p != z)
+            def _():
+                to_col(p).start()
 
         landed(crecv2, rsc.at[1]).wait()
         cyc = csend2[g]
         for k in range(1, grps):
             cyc = cyc + crecv2[k - 1]
         extra[...] = cyc
-        for t, (ref, own) in enumerate(((send1, njs), (csend1, 1), (send2, 1), (csend2, 1))):
-            landed(ref.at[pl.ds(0, ref.shape[0] - own)], sent.at[t]).wait()
-        landed(recv2, rs2).wait()
+        def all_sent(t, ref, count):
+            landed(ref.at[pl.ds(0, count)], sent.at[t]).wait()
+
+        @pl.when(source)
+        def _():
+            all_sent(0, send1, (excs - 1) * (njs - 1))
+            all_sent(2, send2, cols - 1 - blocks)
+            all_sent(4, direct, excs * blocks)
+
+        @pl.when(jnp.logical_not(source))
+        def _():
+            all_sent(0, send1, (excs - 1) * njs)
+            all_sent(2, send2, cols - 1)
+
+        all_sent(1, csend1, excs - 1)
+        all_sent(3, csend2, grps - 1)
+
+        @pl.when(target)
+        def _():
+            landed(recv2.at[pl.ds(0, cols - 1 - blocks)], rs2).wait()
+            landed(direct, rsd).wait()
+            for t in range(blocks):
+                plane = direct[t * excs]
+                for k in range(1, excs):
+                    plane = plane + direct[t * excs + k]
+                recv2[lax.rem(z - (half + t) - 1 + cols, cols)] = plane
+
+        @pl.when(jnp.logical_not(target))
+        def _():
+            landed(recv2, rs2).wait()
+
         result = send2[z]
         for k in range(1, cols):
             result = result + recv2[k - 1]
@@ -189,13 +260,15 @@
             pltpu.VMEM((cols - 1, NI, 128), F32),
             pltpu.VMEM((grps, NI, 128), F32),
             pltpu.VMEM((grps - 1, NI, 128), F32),
+            pltpu.VMEM((excs * blocks, NI, 128), F32),
             DMA,
             DMA((virts // 2,)),
             DMA((len(GROUPS),)),
             DMA((2,)),
-            DMA((4,)),
+            DMA((5,)),
             DMA((njs,)),
             DMA((2,)),
+            DMA,
             DMA,
             pltpu.SemaphoreType.REGULAR,
         ]

time: 41.2 us -> 39.3 us (0.954); the launches traced: 40.4 us -> 39.1 us
  Pallas kernels: 39.8 us -> 38.6 us
    pallas_call x1, Pallas kernels: 39.8 us -> 38.6 us  [shards(): pl.pallas_call(make_kernel(grps, excs, cols), out_shape=(pltpu.VMEM((NI,...]
where the time goes in v3:
time: 39.3 us; the launch traced here: 39.1 us
  Pallas kernels  38.6 us (98%)
  other arithmetic  0.57 us (1%)
    pallas_call x1, Pallas kernels, shards(): pl.pallas_call(make_kernel(grps, excs, cols), out_shape=(pltpu.VMEM((NI,...  38.6 us

profile of v3, /device:TPU:1, one launch (start us, length us, event | category | flops | bytes accessed | tf_op | source)
XLA Modules:
  0.0 39.1 jit_solution(17560267730099380180)
XLA Ops:
  0.0 38.6 %residual.1 = (f32[2,128]{1,0:T(2,128)S(1)}, f32[2,128]{1,0:T(2,128)S(1)}) custom-call(f32[128,8,512]{2,1,0:T(8,128)} %window.1, f32[128,16,512]{2,1,0:T(8,128)} %fitted.1, f32[16,16,512]{2,1,0:T(8,128)} %amps.1, f32[64,1024]{1,0:T(8,128)} %cycle.1, f32[1024,128]{1,0:T(8,128)} %panel.1), custom_call_target="tpu_custom_call" | custom-call | tf_op jit(solution)/shard_map/residual/pallas_call | solution.py:276
  38.6 0.6 %add.3 = f32[2,128]{1,0:T(2,128)} add(f32[2,128]{1,0:T(2,128)S(1)} %get-tuple-element.7, f32[2,128]{1,0:T(2,128)S(1)} %get-tuple-element.8) | non-fusion elementwise | flops 256 | bytes 3072 | tf_op jit(solution)/shard_map/add | solution.py:285

commit v4 on v3

--- a/solution.py
+++ b/solution.py
@@ -9,7 +9,7 @@
 F32 = jnp.float32
 BF16 = jnp.bfloat16
 NI = 2
-GROUPS = ((0, 4), (4, 4), (8, 4), (12, 2), (14, 2))
+GROUPS = ((0, 10), (10, 6))
 ORDER = (0, 1, 7, 2, 6, 3, 5, 4)
 
 
@@ -43,7 +43,7 @@
         for d in range(fits):
             pltpu.make_async_copy(amps.at[:, d, :], ab.at[pl.ds(d * pairs, pairs), :], amp_load).start()
         for a in range(virts):
-            pltpu.make_async_copy(window.at[:, a, :], wb.at[pl.ds(a * aux, aux), :], win_load.at[a // 2]).start()
+            pltpu.make_async_copy(window.at[:, a, :], wb.at[pl.ds(a * aux, aux), :], win_load).start()
         for t, (d0, nd) in enumerate(GROUPS):
             for d in range(d0, d0 + nd):
                 pltpu.make_async_copy(fitted.at[:, d, :], fb.at[pl.ds(d * aux, aux), :], fit_load.at[t]).start()
@@ -74,10 +74,10 @@
                 pl.semaphore_signal(barrier, inc=1, device_id={"col": p}, device_id_type=MESH)
 
         landed(ab, amp_load).wait()
+        landed(wb, win_load).wait()
         amp = halves(ab[...])
         for a in range(0, virts, 2):
             both = pl.ds(a * aux, 2 * aux)
-            landed(wb.at[both, :], win_load.at[a // 2]).wait()
             inner = product(amp, halves(wb[both, :]), ((1,), (1,)))
             for s in range(2):
                 for d in range(fits):
@@ -85,6 +85,12 @@
                     rows, lanes = pl.ds((a + s) * pairs, pairs), pl.ds(d * aux, aux)
                     lh[rows, lanes] = high
                     ll[rows, lanes] = low
+
+        pl.semaphore_wait(barrier, len(near) + known + jnp.where(source, (excs - 1) * blocks, 0))
+
+        @pl.loop(0, known)
+        def _(p):
+            pl.semaphore_signal(ready, inc=1, device_id={"col": p}, device_id_type=MESH)
 
         for t, (d0, nd) in enumerate(GROUPS):
             deep = pl.ds(d0 * aux, nd * aux)
@@ -103,8 +109,6 @@
                             row = q * pairs + i * njs
                             send1[pl.ds(q * njs, njs), (n + s) * NI + i, :] = terms[row : row + njs, s * 128 : (s + 1) * 128]
 
-        pl.semaphore_wait(barrier, len(near) + known + jnp.where(source, (excs - 1) * blocks, 0))
-
         @pl.when(source)
         def _():
             for t in range(blocks):
@@ -125,10 +129,6 @@
 
         for p in range(1, njs):
             to_exc(p, js[p])
-
-        @pl.loop(0, known)
-        def _(p):
-            pl.semaphore_signal(ready, inc=1, device_id={"col": p}, device_id_type=MESH)
 
         landed(cb, cyc_load.at[0]).wait()
         landed(pb, cyc_load.at[1]).wait()
@@ -262,7 +262,7 @@
             pltpu.VMEM((grps - 1, NI, 128), F32),
             pltpu.VMEM((excs * blocks, NI, 128), F32),
             DMA,
-            DMA((virts // 2,)),
+            DMA,
             DMA((len(GROUPS),)),
             DMA((2,)),
             DMA((5,)),

time: 39.3 us -> 40.5 us (1.031)
  the two profiles are of different devices: /device:TPU:1 before, /device:TPU:2 now
where the time goes in v4:
time: 40.5 us; the launch traced here: 40.4 us
  Pallas kernels  39.8 us (98%)
  other arithmetic  0.57 us (1%)
    pallas_call x1, Pallas kernels, shards(): pl.pallas_call(make_kernel(grps, excs, cols), out_shape=(pltpu.VMEM((NI,...  39.8 us

profile of v4, /device:TPU:2, one launch (start us, length us, event | category | flops | bytes accessed | tf_op | source)
XLA Modules:
  0.0 40.4 jit_solution(498215856350351617)
XLA Ops:
  0.0 39.8 %residual.1 = (f32[2,128]{1,0:T(2,128)S(1)}, f32[2,128]{1,0:T(2,128)S(1)}) custom-call(f32[128,8,512]{2,1,0:T(8,128)} %window.1, f32[128,16,512]{2,1,0:T(8,128)} %fitted.1, f32[16,16,512]{2,1,0:T(8,128)} %amps.1, f32[64,1024]{1,0:T(8,128)} %cycle.1, f32[1024,128]{1,0:T(8,128)} %panel.1), custom_call_target="tpu_custom_call" | custom-call | tf_op jit(solution)/shard_map/residual/pallas_call | solution.py:276
  39.8 0.6 %add.3 = f32[2,128]{1,0:T(2,128)} add(f32[2,128]{1,0:T(2,128)S(1)} %get-tuple-element.7, f32[2,128]{1,0:T(2,128)S(1)} %get-tuple-element.8) | non-fusion elementwise | flops 256 | bytes 3072 | tf_op jit(solution)/shard_map/add | solution.py:285

commit v5 on v4

--- a/solution.py
+++ b/solution.py
@@ -85,12 +85,6 @@
                     rows, lanes = pl.ds((a + s) * pairs, pairs), pl.ds(d * aux, aux)
                     lh[rows, lanes] = high
                     ll[rows, lanes] = low
-
-        pl.semaphore_wait(barrier, len(near) + known + jnp.where(source, (excs - 1) * blocks, 0))
-
-        @pl.loop(0, known)
-        def _(p):
-            pl.semaphore_signal(ready, inc=1, device_id={"col": p}, device_id_type=MESH)
 
         for t, (d0, nd) in enumerate(GROUPS):
             deep = pl.ds(d0 * aux, nd * aux)
@@ -109,6 +103,8 @@
                             row = q * pairs + i * njs
                             send1[pl.ds(q * njs, njs), (n + s) * NI + i, :] = terms[row : row + njs, s * 128 : (s + 1) * 128]
 
+        pl.semaphore_wait(barrier, len(near) + known + jnp.where(source, (excs - 1) * blocks, 0))
+
         @pl.when(source)
         def _():
             for t in range(blocks):
@@ -129,6 +125,10 @@
 
         for p in range(1, njs):
             to_exc(p, js[p])
+
+        @pl.loop(0, known)
+        def _(p):
+            pl.semaphore_signal(ready, inc=1, device_id={"col": p}, device_id_type=MESH)
 
         landed(cb, cyc_load.at[0]).wait()
         landed(pb, cyc_load.at[1]).wait()

time: 40.5 us -> 39.1 us (0.965)
  the two profiles are of different devices: /device:TPU:2 before, /device:TPU:1 now
where the time goes in v5:
time: 39.1 us; the launch traced here: 38.5 us
  Pallas kernels  37.9 us (97%)
  other arithmetic  0.57 us (1%)
    pallas_call x1, Pallas kernels, shards(): pl.pallas_call(make_kernel(grps, excs, cols), out_shape=(pltpu.VMEM((NI,...  37.9 us

profile of v5, /device:TPU:1, one launch (start us, length us, event | category | flops | bytes accessed | tf_op | source)
XLA Modules:
  0.0 38.5 jit_solution(16193465382946553500)
XLA Ops:
  0.0 37.9 %residual.1 = (f32[2,128]{1,0:T(2,128)S(1)}, f32[2,128]{1,0:T(2,128)S(1)}) custom-call(f32[128,8,512]{2,1,0:T(8,128)} %window.1, f32[128,16,512]{2,1,0:T(8,128)} %fitted.1, f32[16,16,512]{2,1,0:T(8,128)} %amps.1, f32[64,1024]{1,0:T(8,128)} %cycle.1, f32[1024,128]{1,0:T(8,128)} %panel.1), custom_call_target="tpu_custom_call" | custom-call | tf_op jit(solution)/shard_map/residual/pallas_call | solution.py:276
  37.9 0.6 %add.3 = f32[2,128]{1,0:T(2,128)} add(f32[2,128]{1,0:T(2,128)S(1)} %get-tuple-element.7, f32[2,128]{1,0:T(2,128)S(1)} %get-tuple-element.8) | non-fusion elementwise | flops 256 | bytes 3072 | tf_op jit(solution)/shard_map/add | solution.py:285

commit v6 on v5

--- a/solution.py
+++ b/solution.py
@@ -10,7 +10,6 @@
 BF16 = jnp.bfloat16
 NI = 2
 GROUPS = ((0, 10), (10, 6))
-ORDER = (0, 1, 7, 2, 6, 3, 5, 4)
 
 
 def halves(x):
@@ -112,19 +111,17 @@
                     pltpu.make_async_remote_copy(send1.at[(e ^ k) * njs, pl.ds(t * NI, NI), :], direct.at[(z - half) * excs + e],
                                                  sent.at[4], rsd, device_id={"exc": e ^ k, "col": t}, device_id_type=MESH).start()
 
-        def to_exc(p, j):
+        def to_exc(j):
             for k in reversed(range(1, excs)):
-                pltpu.make_async_remote_copy(send1.at[(e ^ k) * njs + j], recv1.at[p, k - 1], sent.at[0], rs1.at[p],
+                pltpu.make_async_remote_copy(send1.at[(e ^ k) * njs + j], recv1.at[j, k - 1], sent.at[0], rs1.at[j],
                                              device_id={"exc": e ^ k}, device_id_type=MESH).start()
 
-        js = [lax.rem(z // blocks + (njs // 2 + t), njs) for t in ORDER]
-
         @pl.when(jnp.logical_not(source))
         def _():
-            to_exc(0, js[0])
+            to_exc(0)
 
         for p in range(1, njs):
-            to_exc(p, js[p])
+            to_exc(p)
 
         @pl.loop(0, known)
         def _(p):
@@ -145,11 +142,11 @@
             return pltpu.make_async_remote_copy(send2.at[p], recv2.at[lax.rem(p - z - 1 + cols, cols)], sent.at[2], rs2,
                                                 device_id={"col": p}, device_id_type=MESH)
 
-        def reduce_to_cols(p, j):
-            landed(recv1.at[p], rs1.at[p]).wait()
+        def reduce_to_cols(j):
+            landed(recv1.at[j], rs1.at[j]).wait()
             total = send1[e * njs + j]
             for k in range(1, excs):
-                total = total + recv1[p, k - 1]
+                total = total + recv1[j, k - 1]
             for n in range(blocks):
                 to = j * blocks + n
                 send2[to] = total[n * NI : (n + 1) * NI, :]
@@ -160,10 +157,10 @@
 
         @pl.when(jnp.logical_not(source))
         def _():
-            reduce_to_cols(0, js[0])
+            reduce_to_cols(0)
 
         for p in range(1, njs):
-            reduce_to_cols(p, js[p])
+            reduce_to_cols(p)
 
         landed(crecv1, rsc.at[0]).wait()
         total = csend1[e]

time: 39.1 us -> 39.1 us (level)
  no operation moved by 1% of the time
where the time goes in v6:
time: 39.1 us; the launch traced here: 38.4 us
  Pallas kernels  37.8 us (97%)
  other arithmetic  0.57 us (1%)
    pallas_call x1, Pallas kernels, shards(): pl.pallas_call(make_kernel(grps, excs, cols), out_shape=(pltpu.VMEM((NI,...  37.8 us

profile of v6, /device:TPU:1, one launch (start us, length us, event | category | flops | bytes accessed | tf_op | source)
XLA Modules:
  0.0 38.4 jit_solution(17048376737071786788)
XLA Ops:
  0.0 37.8 %residual.1 = (f32[2,128]{1,0:T(2,128)S(1)}, f32[2,128]{1,0:T(2,128)S(1)}) custom-call(f32[128,8,512]{2,1,0:T(8,128)} %window.1, f32[128,16,512]{2,1,0:T(8,128)} %fitted.1, f32[16,16,512]{2,1,0:T(8,128)} %amps.1, f32[64,1024]{1,0:T(8,128)} %cycle.1, f32[1024,128]{1,0:T(8,128)} %panel.1), custom_call_target="tpu_custom_call" | custom-call | tf_op jit(solution)/shard_map/residual/pallas_call | solution.py:273
  37.8 0.6 %add.3 = f32[2,128]{1,0:T(2,128)} add(f32[2,128]{1,0:T(2,128)S(1)} %get-tuple-element.7, f32[2,128]{1,0:T(2,128)S(1)} %get-tuple-element.8) | non-fusion elementwise | flops 256 | bytes 3072 | tf_op jit(solution)/shard_map/add | solution.py:282
